TPU v7x, 32 devices: a whole 2x2x4 slice. The times are simulated.
32 devices in a mesh: south: 4 (over z), east: 4 (over y, x), down: 2 (over core).
Axes of the slice: x: 2, y: 2, z: 4, core: 2. Of those that a mesh axis runs over, the one named last changes fastest.
Arguments:
- initial_scalar_state: float32 [16, 128, 256, 128], P('south', 'east', 'down'), may hold values from 0.2 to 1.8
- scaled_wind_second: float32 [16, 128, 256, 128], P('south', 'east', 'down'), may hold values from -0.3 to 0.3
- scaled_wind_first: float32 [16, 128, 256, 128], P('south', 'east', 'down'), may hold values from -0.3 to 0.3
- scaled_wind_third: float32 [16, 128, 256, 128], P('south', 'east', 'down'), may hold values from -0.3 to 0.3
Outputs:
- temperature_end: float32 [16, 128, 256, 128], P('south', 'east', 'down')
All inputs are finite; a program needn't handle non-finite values.
Results may differ from a plain program's by a relative error of at most 0.00002.
Values sent between devices are 32-bit elements; how exact they have to be, the bound alone decides.
A program may use at most 448 MiB of HBM per device.

v0:
```python
import jax
import jax.numpy as jnp
from jax import lax
from jax.sharding import PartitionSpec as P

STEPS = 4


def padded(array, sides, width):
    for axis, dim in sides:
        size, length = (lax.axis_size(axis), array.shape[dim])
        up = [(i, (i + 1) % size) for i in range(size)]
        down = [(j, i) for i, j in up]
        last = lax.slice_in_dim(array, length - width, length, axis=dim)
        leading = lax.slice_in_dim(array, 0, width, axis=dim)
        before = lax.ppermute(last, axis, up)
        after = lax.ppermute(leading, axis, down)
        array = jnp.concatenate([before, array, after], axis=dim)
    return array


def strip_edges(values, dims):
    for dim in dims:
        values = lax.slice_in_dim(values, 1, values.shape[dim] - 1, axis=dim)
    return values


def neighbour(values, dim, start, dims):
    others = [other for other in dims if other != dim]
    values = strip_edges(values, others)
    return lax.slice_in_dim(values, start, start + values.shape[dim] - 2, axis=dim)


def update_lone_timestep(
    padded_with_margin, scaled_wind_second, scaled_wind_first, scaled_wind_third
):
    middle = strip_edges(padded_with_margin, (0, 1, 2))
    lower = [neighbour(padded_with_margin, dim, 0, (0, 1, 2)) for dim in (0, 1, 2)]
    upper = [neighbour(padded_with_margin, dim, 2, (0, 1, 2)) for dim in (0, 1, 2)]
    slopes = [above - below for above, below in zip(upper, lower)]
    smooth_rate = 0.05
    spread = lower[0] + upper[0] + lower[1] + upper[1] + lower[2] + upper[2] - 6.0 * middle
    return (
        middle
        - scaled_wind_second * slopes[0]
        - scaled_wind_first * slopes[1]
        - scaled_wind_third * slopes[2]
        + smooth_rate * spread
    )


def on_device(initial_scalar_state, scaled_wind_second, scaled_wind_first, scaled_wind_third):
    for step in range(STEPS):
        padded_with_margin = padded(
            initial_scalar_state, (("south", 0), ("east", 1), ("down", 2)), 1
        )
        initial_scalar_state = update_lone_timestep(
            padded_with_margin, scaled_wind_second, scaled_wind_first, scaled_wind_third
        )
    return initial_scalar_state


def solution(mesh):
    placed = (
        P("south", "east", "down", None),
        P("south", "east", "down", None),
        P("south", "east", "down", None),
        P("south", "east", "down", None),
    )
    return jax.shard_map(
        on_device,
        mesh=mesh,
        in_specs=placed,
        out_specs=P("south", "east", "down", None),
        check_vma=False,
    )
```

profile of v0, /device:TPU:0, one launch (start us, length us, event | category | flops | bytes accessed | tf_op | source)
XLA Modules:
  0.0 603.3 jit_solution(13474058437822647948)
XLA Ops:
  0.0 4.1 fusion.4
  4.1 3.1 collective-permute-start.1
  7.1 2.0 collective-permute-start
  9.2 46.5 %collective-permute-done.1 = f32[1,32,128,128]{3,2,1,0:T(8,128)S(1)} collective-permute-done((f32[1,32,128,128]{3,2,1,0:T(8,128)S(1)}, f32[1,32,128,128]{3,2,1,0:T(8,128)S(1)}, u32[]{:S(2)}, u32[]{:S(2)}) %collective-permute-start.1) | collective-permute-done | bytes 2097184 | tf_op jit(solution)/shard_map/ppermute | solution.py:16
  55.7 1.3 copy-done.8
  57.2 1.1 constant_dynamic-update-slice_fusion.1
  58.3 41.2 %collective-permute-done = f32[1,32,128,128]{3,2,1,0:T(8,128)} collective-permute-done((f32[1,32,128,128]{3,2,1,0:T(8,128)}, f32[1,32,128,128]{3,2,1,0:T(8,128)}, u32[]{:S(2)}, u32[]{:S(2)}) %collective-permute-start) | collective-permute-done | bytes 2097184 | tf_op jit(solution)/shard_map/ppermute | solution.py:17
  99.5 1.7 constant_dynamic-update-slice_fusion
  101.3 1.5 collective-permute-start.3
  102.8 1.4 collective-permute-start.2
  104.3 10.0 %collective-permute-done.3 = f32[6,1,128,128]{3,2,1,0:T(8,128)S(1)} collective-permute-done((f32[6,1,128,128]{3,2,1,0:T(8,128)S(1)}, f32[6,1,128,128]{3,2,1,0:T(8,128)S(1)}, u32[]{:S(2)}, u32[]{:S(2)}) %collective-permute-start.3) | collective-permute-done | bytes 393248 | tf_op jit(solution)/shard_map/ppermute | solution.py:16
  114.2 7.2 %collective-permute-done.2 = f32[6,1,128,128]{3,2,1,0:T(8,128)S(1)} collective-permute-done((f32[6,1,128,128]{3,2,1,0:T(8,128)S(1)}, f32[6,1,128,128]{3,2,1,0:T(8,128)S(1)}, u32[]{:S(2)}, u32[]{:S(2)}) %collective-permute-start.2) | collective-permute-done | bytes 393248 | tf_op jit(solution)/shard_map/ppermute | solution.py:17
  121.7 0.6 collective-permute-start.5
  122.2 0.7 collective-permute-done.4
  123.3 31.4 %multiply_add_fusion.3 = f32[4,32,128,128]{3,2,1,0:T(8,128)} fusion(f32[4,32,128,128]{3,2,1,0:T(8,128)} %param.4, f32[4,32,128,128]{3,2,1,0:T(8,128)} %param.7, f32[6,34,1,128]{3,2,1,0:T(1,128)S(1)} %copy.26, f32[6,1,128,128]{3,2,1,0:T(8,128)S(1)} %collective-permute-done.2, f32[6,32,128,128]{3,2,1,0:T(8,128)} %copy-done.3, ...), kind=kLoop, calls=%fused_computation.67 | loop fusion | flops 58720256 | bytes 59715584 | tf_op jit(solution)/shard_map/add | solution.py:44
  154.8 2.6 fusion.3
  157.4 1.3 collective-permute-start.7
  158.7 2.6 collective-permute-start.6
  161.3 46.5 %collective-permute-done.7 = f32[1,32,128,128]{3,2,1,0:T(8,128)S(1)} collective-permute-done((f32[1,32,128,128]{3,2,1,0:T(8,128)S(1)}, f32[1,32,128,128]{3,2,1,0:T(8,128)S(1)}, u32[]{:S(2)}, u32[]{:S(2)}) %collective-permute-start.7) | collective-permute-done | bytes 2097184 | tf_op jit(solution)/shard_map/ppermute | solution.py:16
  207.8 43.5 %collective-permute-done.6 = f32[1,32,128,128]{3,2,1,0:T(8,128)S(1)} collective-permute-done((f32[1,32,128,128]{3,2,1,0:T(8,128)S(1)}, f32[1,32,128,128]{3,2,1,0:T(8,128)S(1)}, u32[]{:S(2)}, u32[]{:S(2)}) %collective-permute-start.6) | collective-permute-done | bytes 2097184 | tf_op jit(solution)/shard_map/ppermute | solution.py:17
  251.3 1.5 collective-permute-start.9
  252.9 1.4 collective-permute-start.8
  254.3 10.0 %collective-permute-done.9 = f32[6,1,128,128]{3,2,1,0:T(8,128)S(1)} collective-permute-done((f32[6,1,128,128]{3,2,1,0:T(8,128)S(1)}, f32[6,1,128,128]{3,2,1,0:T(8,128)S(1)}, u32[]{:S(2)}, u32[]{:S(2)}) %collective-permute-start.9) | collective-permute-done | bytes 393248 | tf_op jit(solution)/shard_map/ppermute | solution.py:16
  264.3 5.7 collective-permute-done.8
  270.9 0.7 collective-permute-done.10
  271.9 31.6 %multiply_add_fusion.2 = f32[4,32,128,128]{3,2,1,0:T(8,128)} fusion(f32[4,32,128,128]{3,2,1,0:T(8,128)} %multiply_add_fusion.3, f32[4,32,128,128]{3,2,1,0:T(8,128)} %param.7, f32[6,34,1,128]{3,2,1,0:T(1,128)S(1)} %copy.30, f32[6,1,128,128]{3,2,1,0:T(8,128)S(1)} %collective-permute-done.8, f32[1,32,128,128]{3,2,1,0:T(8,128)} %copy-done.5, ...), kind=kLoop, calls=%fused_computation.66 | loop fusion | flops 75497472 | bytes 47132672 | tf_op jit(solution)/shard_map/add | solution.py:44
  303.5 2.6 fusion.2
  306.2 0.7 collective-permute-start.13
  306.8 3.2 collective-permute-start.12
  310.1 46.5 %collective-permute-done.13 = f32[1,32,128,128]{3,2,1,0:T(8,128)S(1)} collective-permute-done((f32[1,32,128,128]{3,2,1,0:T(8,128)S(1)}, f32[1,32,128,128]{3,2,1,0:T(8,128)S(1)}, u32[]{:S(2)}, u32[]{:S(2)}) %collective-permute-start.13) | collective-permute-done | bytes 2097184 | tf_op jit(solution)/shard_map/ppermute | solution.py:16
  356.6 42.8 %collective-permute-done.12 = f32[1,32,128,128]{3,2,1,0:T(8,128)S(1)} collective-permute-done((f32[1,32,128,128]{3,2,1,0:T(8,128)S(1)}, f32[1,32,128,128]{3,2,1,0:T(8,128)S(1)}, u32[]{:S(2)}, u32[]{:S(2)}) %collective-permute-start.12) | collective-permute-done | bytes 2097184 | tf_op jit(solution)/shard_map/ppermute | solution.py:17
  399.5 1.7 collective-permute-start.15
  401.2 1.4 collective-permute-start.14
  402.6 10.0 %collective-permute-done.15 = f32[6,1,128,128]{3,2,1,0:T(8,128)S(1)} collective-permute-done((f32[6,1,128,128]{3,2,1,0:T(8,128)S(1)}, f32[6,1,128,128]{3,2,1,0:T(8,128)S(1)}, u32[]{:S(2)}, u32[]{:S(2)}) %collective-permute-start.15) | collective-permute-done | bytes 393248 | tf_op jit(solution)/shard_map/ppermute | solution.py:16
  412.6 6.7 %collective-permute-done.14 = f32[6,1,128,128]{3,2,1,0:T(8,128)S(1)} collective-permute-done((f32[6,1,128,128]{3,2,1,0:T(8,128)S(1)}, f32[6,1,128,128]{3,2,1,0:T(8,128)S(1)}, u32[]{:S(2)}, u32[]{:S(2)}) %collective-permute-start.14) | collective-permute-done | bytes 393248 | tf_op jit(solution)/shard_map/ppermute | solution.py:17
  420.1 0.7 collective-permute-done.16
  421.2 31.6 %multiply_add_fusion.1 = f32[4,32,128,128]{3,2,1,0:T(8,128)} fusion(f32[4,32,128,128]{3,2,1,0:T(8,128)} %multiply_add_fusion.2, f32[4,32,128,128]{3,2,1,0:T(8,128)} %param.7, f32[6,34,1,128]{3,2,1,0:T(1,128)S(1)} %copy.34, f32[6,1,128,128]{3,2,1,0:T(8,128)S(1)} %collective-permute-done.14, f32[1,32,128,128]{3,2,1,0:T(8,128)} %copy-done.6, ...), kind=kLoop, calls=%fused_computation.65 | loop fusion | flops 75497472 | bytes 47132672 | tf_op jit(solution)/shard_map/add | solution.py:44
  452.9 2.6 fusion.1
  455.5 2.1 collective-permute-start.19
  457.6 1.8 collective-permute-start.18
  459.4 46.5 %collective-permute-done.19 = f32[1,32,128,128]{3,2,1,0:T(8,128)S(1)} collective-permute-done((f32[1,32,128,128]{3,2,1,0:T(8,128)S(1)}, f32[1,32,128,128]{3,2,1,0:T(8,128)S(1)}, u32[]{:S(2)}, u32[]{:S(2)}) %collective-permute-start.19) | collective-permute-done | bytes 2097184 | tf_op jit(solution)/shard_map/ppermute | solution.py:16
  505.9 44.3 %collective-permute-done.18 = f32[1,32,128,128]{3,2,1,0:T(8,128)S(1)} collective-permute-done((f32[1,32,128,128]{3,2,1,0:T(8,128)S(1)}, f32[1,32,128,128]{3,2,1,0:T(8,128)S(1)}, u32[]{:S(2)}, u32[]{:S(2)}) %collective-permute-start.18) | collective-permute-done | bytes 2097184 | tf_op jit(solution)/shard_map/ppermute | solution.py:17
  550.2 1.5 collective-permute-start.21
  551.8 1.4 collective-permute-start.20
  553.2 10.0 %collective-permute-done.21 = f32[6,1,128,128]{3,2,1,0:T(8,128)S(1)} collective-permute-done((f32[6,1,128,128]{3,2,1,0:T(8,128)S(1)}, f32[6,1,128,128]{3,2,1,0:T(8,128)S(1)}, u32[]{:S(2)}, u32[]{:S(2)}) %collective-permute-start.21) | collective-permute-done | bytes 393248 | tf_op jit(solution)/shard_map/ppermute | solution.py:16
  563.2 6.5 %collective-permute-done.20 = f32[6,1,128,128]{3,2,1,0:T(8,128)S(1)} collective-permute-done((f32[6,1,128,128]{3,2,1,0:T(8,128)S(1)}, f32[6,1,128,128]{3,2,1,0:T(8,128)S(1)}, u32[]{:S(2)}, u32[]{:S(2)}) %collective-permute-start.20) | collective-permute-done | bytes 393248 | tf_op jit(solution)/shard_map/ppermute | solution.py:17
  570.5 0.7 collective-permute-done.22
  571.6 31.5 %multiply_add_fusion = f32[4,32,128,128]{3,2,1,0:T(8,128)} fusion(f32[4,32,128,128]{3,2,1,0:T(8,128)} %multiply_add_fusion.1, f32[4,32,128,128]{3,2,1,0:T(8,128)} %param.7, f32[6,34,1,128]{3,2,1,0:T(1,128)S(1)} %copy.38, f32[6,1,128,128]{3,2,1,0:T(8,128)S(1)} %collective-permute-done.20, f32[1,32,128,128]{3,2,1,0:T(8,128)} %copy-done.7, ...), kind=kLoop, calls=%fused_computation.64 | loop fusion | flops 75497472 | bytes 47132672 | tf_op jit(solution)/shard_map/add | solution.py:44
  (55 shorter events, 4.4 us)
Async XLA Ops:
  0.0 57.2 %copy-start.4 = (f32[4,32,128,128]{3,2,1,0:T(8,128)S(1)}, f32[4,32,128,128]{3,2,1,0:T(8,128)}, u32[]{:S(2)}) copy-start(f32[4,32,128,128]{3,2,1,0:T(8,128)} %param.4) | copy-start | bytes 25165828
  4.1 51.6 %collective-permute-start.1 = (f32[1,32,128,128]{3,2,1,0:T(8,128)S(1)}, f32[1,32,128,128]{3,2,1,0:T(8,128)S(1)}, u32[]{:S(2)}, u32[]{:S(2)}) collective-permute-start(f32[1,32,128,128]{3,2,1,0:T(8,128)S(1)} %get-tuple-element.28), channel_id=1, source_target_pairs={{0,8},{8,16},{16,24},{24,0},{1,9},{9,17},{17,25},{25,1},{2,10},{10... | collective-permute-start | bytes 6291464 | tf_op jit(solution)/shard_map/ppermute | solution.py:16
  7.1 92.3 %collective-permute-start = (f32[1,32,128,128]{3,2,1,0:T(8,128)}, f32[1,32,128,128]{3,2,1,0:T(8,128)}, u32[]{:S(2)}, u32[]{:S(2)}) collective-permute-start(f32[1,32,128,128]{3,2,1,0:T(8,128)} %get-tuple-element.27), channel_id=1, source_target_pairs={{8,0},{16,8},{24,16},{0,24},{9,1},{17,9},{25,17},{1,25},{10,2},{18... | collective-permute-start | bytes 6291464 | tf_op jit(solution)/shard_map/ppermute | solution.py:17
  55.7 1.3 copy-start.8
  101.2 20.2 %copy-start.3 = (f32[6,32,128,128]{3,2,1,0:T(8,128)}, f32[6,32,128,128]{3,2,1,0:T(8,128)S(1)}, u32[]{:S(2)}) copy-start(f32[6,32,128,128]{3,2,1,0:T(8,128)S(1)} %constant_dynamic-update-slice_fusion) | copy-start | bytes 37748740
  101.2 22.1 %copy-start.9 = (f32[1,32,128,128]{3,2,1,0:T(8,128)S(1)}, f32[1,32,128,128]{3,2,1,0:T(8,128)}, u32[]{:S(2)}) copy-start(f32[1,32,128,128]{3,2,1,0:T(8,128)} %copy-done.8) | copy-start | bytes 6291460
  101.3 12.9 %collective-permute-start.3 = (f32[6,1,128,128]{3,2,1,0:T(8,128)S(1)}, f32[6,1,128,128]{3,2,1,0:T(8,128)S(1)}, u32[]{:S(2)}, u32[]{:S(2)}) collective-permute-start(f32[6,1,128,128]{3,2,1,0:T(8,128)S(1)} %get-tuple-element.19), channel_id=1, source_target_pairs={{0,2},{2,4},{4,6},{6,0},{1,3},{3,5},{5,7},{7,1},{8,10},{10,12},{12... | collective-permute-start | bytes 1179656 | tf_op jit(solution)/shard_map/ppermute | solution.py:16
  102.8 18.6 %collective-permute-start.2 = (f32[6,1,128,128]{3,2,1,0:T(8,128)S(1)}, f32[6,1,128,128]{3,2,1,0:T(8,128)S(1)}, u32[]{:S(2)}, u32[]{:S(2)}) collective-permute-start(f32[6,1,128,128]{3,2,1,0:T(8,128)S(1)} %get-tuple-element.20), channel_id=1, source_target_pairs={{2,0},{4,2},{6,4},{0,6},{3,1},{5,3},{7,5},{1,7},{10,8},{12,10},{14... | collective-permute-start | bytes 1179656 | tf_op jit(solution)/shard_map/ppermute | solution.py:17
  121.6 1.4 collective-permute-start.4
  121.7 1.5 collective-permute-start.5
  154.8 96.5 %copy-start = (f32[4,32,128,128]{3,2,1,0:T(8,128)S(1)}, f32[4,32,128,128]{3,2,1,0:T(8,128)}, u32[]{:S(2)}) copy-start(f32[4,32,128,128]{3,2,1,0:T(8,128)} %multiply_add_fusion.3) | copy-start | bytes 25165828
  157.4 50.4 %collective-permute-start.7 = (f32[1,32,128,128]{3,2,1,0:T(8,128)S(1)}, f32[1,32,128,128]{3,2,1,0:T(8,128)S(1)}, u32[]{:S(2)}, u32[]{:S(2)}) collective-permute-start(f32[1,32,128,128]{3,2,1,0:T(8,128)S(1)} %get-tuple-element.25), channel_id=1, source_target_pairs={{0,8},{8,16},{16,24},{24,0},{1,9},{9,17},{17,25},{25,1},{2,10},{10... | collective-permute-start | bytes 6291464 | tf_op jit(solution)/shard_map/ppermute | solution.py:16
  158.7 92.6 %collective-permute-start.6 = (f32[1,32,128,128]{3,2,1,0:T(8,128)S(1)}, f32[1,32,128,128]{3,2,1,0:T(8,128)S(1)}, u32[]{:S(2)}, u32[]{:S(2)}) collective-permute-start(f32[1,32,128,128]{3,2,1,0:T(8,128)S(1)} %get-tuple-element.26), channel_id=1, source_target_pairs={{8,0},{16,8},{24,16},{0,24},{9,1},{17,9},{25,17},{1,25},{10,2},{18... | collective-permute-start | bytes 6291464 | tf_op jit(solution)/shard_map/ppermute | solution.py:17
  251.3 18.9 %copy-start.5 = (f32[1,32,128,128]{3,2,1,0:T(8,128)}, f32[1,32,128,128]{3,2,1,0:T(8,128)S(1)}, u32[]{:S(2)}) copy-start(f32[1,32,128,128]{3,2,1,0:T(8,128)S(1)} %collective-permute-done.6) | copy-start | bytes 6291460
  251.3 12.9 %collective-permute-start.9 = (f32[6,1,128,128]{3,2,1,0:T(8,128)S(1)}, f32[6,1,128,128]{3,2,1,0:T(8,128)S(1)}, u32[]{:S(2)}, u32[]{:S(2)}) collective-permute-start(f32[6,1,128,128]{3,2,1,0:T(8,128)S(1)} %get-tuple-element.17), channel_id=1, source_target_pairs={{0,2},{2,4},{4,6},{6,0},{1,3},{3,5},{5,7},{7,1},{8,10},{10,12},{12... | collective-permute-start | bytes 1179656 | tf_op jit(solution)/shard_map/ppermute | solution.py:16
  252.9 17.1 %collective-permute-start.8 = (f32[6,1,128,128]{3,2,1,0:T(8,128)S(1)}, f32[6,1,128,128]{3,2,1,0:T(8,128)S(1)}, u32[]{:S(2)}, u32[]{:S(2)}) collective-permute-start(f32[6,1,128,128]{3,2,1,0:T(8,128)S(1)} %get-tuple-element.18), channel_id=1, source_target_pairs={{2,0},{4,2},{6,4},{0,6},{3,1},{5,3},{7,5},{1,7},{10,8},{12,10},{14... | collective-permute-start | bytes 1179656 | tf_op jit(solution)/shard_map/ppermute | solution.py:17
  270.2 1.4 collective-permute-start.10
  270.3 1.5 collective-permute-start.11
  303.5 95.9 %copy-start.1 = (f32[4,32,128,128]{3,2,1,0:T(8,128)S(1)}, f32[4,32,128,128]{3,2,1,0:T(8,128)}, u32[]{:S(2)}) copy-start(f32[4,32,128,128]{3,2,1,0:T(8,128)} %multiply_add_fusion.2) | copy-start | bytes 25165828
  306.2 50.4 %collective-permute-start.13 = (f32[1,32,128,128]{3,2,1,0:T(8,128)S(1)}, f32[1,32,128,128]{3,2,1,0:T(8,128)S(1)}, u32[]{:S(2)}, u32[]{:S(2)}) collective-permute-start(f32[1,32,128,128]{3,2,1,0:T(8,128)S(1)} %get-tuple-element.23), channel_id=1, source_target_pairs={{0,8},{8,16},{16,24},{24,0},{1,9},{9,17},{17,25},{25,1},{2,10},{10... | collective-permute-start | bytes 6291464 | tf_op jit(solution)/shard_map/ppermute | solution.py:16
  306.8 92.6 %collective-permute-start.12 = (f32[1,32,128,128]{3,2,1,0:T(8,128)S(1)}, f32[1,32,128,128]{3,2,1,0:T(8,128)S(1)}, u32[]{:S(2)}, u32[]{:S(2)}) collective-permute-start(f32[1,32,128,128]{3,2,1,0:T(8,128)S(1)} %get-tuple-element.24), channel_id=1, source_target_pairs={{8,0},{16,8},{24,16},{0,24},{9,1},{17,9},{25,17},{1,25},{10,2},{18... | collective-permute-start | bytes 6291464 | tf_op jit(solution)/shard_map/ppermute | solution.py:17
  399.4 20.1 %copy-start.6 = (f32[1,32,128,128]{3,2,1,0:T(8,128)}, f32[1,32,128,128]{3,2,1,0:T(8,128)S(1)}, u32[]{:S(2)}) copy-start(f32[1,32,128,128]{3,2,1,0:T(8,128)S(1)} %collective-permute-done.12) | copy-start | bytes 6291460
  399.5 13.1 %collective-permute-start.15 = (f32[6,1,128,128]{3,2,1,0:T(8,128)S(1)}, f32[6,1,128,128]{3,2,1,0:T(8,128)S(1)}, u32[]{:S(2)}, u32[]{:S(2)}) collective-permute-start(f32[6,1,128,128]{3,2,1,0:T(8,128)S(1)} %get-tuple-element.15), channel_id=1, source_target_pairs={{0,2},{2,4},{4,6},{6,0},{1,3},{3,5},{5,7},{7,1},{8,10},{10,12},{12... | collective-permute-start | bytes 1179656 | tf_op jit(solution)/shard_map/ppermute | solution.py:16
  401.2 18.1 %collective-permute-start.14 = (f32[6,1,128,128]{3,2,1,0:T(8,128)S(1)}, f32[6,1,128,128]{3,2,1,0:T(8,128)S(1)}, u32[]{:S(2)}, u32[]{:S(2)}) collective-permute-start(f32[6,1,128,128]{3,2,1,0:T(8,128)S(1)} %get-tuple-element.16), channel_id=1, source_target_pairs={{2,0},{4,2},{6,4},{0,6},{3,1},{5,3},{7,5},{1,7},{10,8},{12,10},{14... | collective-permute-start | bytes 1179656 | tf_op jit(solution)/shard_map/ppermute | solution.py:17
  419.5 1.4 collective-permute-start.16
  419.6 1.5 collective-permute-start.17
  452.8 97.3 %copy-start.2 = (f32[4,32,128,128]{3,2,1,0:T(8,128)S(1)}, f32[4,32,128,128]{3,2,1,0:T(8,128)}, u32[]{:S(2)}) copy-start(f32[4,32,128,128]{3,2,1,0:T(8,128)} %multiply_add_fusion.1) | copy-start | bytes 25165828
  455.5 50.4 %collective-permute-start.19 = (f32[1,32,128,128]{3,2,1,0:T(8,128)S(1)}, f32[1,32,128,128]{3,2,1,0:T(8,128)S(1)}, u32[]{:S(2)}, u32[]{:S(2)}) collective-permute-start(f32[1,32,128,128]{3,2,1,0:T(8,128)S(1)} %get-tuple-element.21), channel_id=1, source_target_pairs={{0,8},{8,16},{16,24},{24,0},{1,9},{9,17},{17,25},{25,1},{2,10},{10... | collective-permute-start | bytes 6291464 | tf_op jit(solution)/shard_map/ppermute | solution.py:16
  457.6 92.6 %collective-permute-start.18 = (f32[1,32,128,128]{3,2,1,0:T(8,128)S(1)}, f32[1,32,128,128]{3,2,1,0:T(8,128)S(1)}, u32[]{:S(2)}, u32[]{:S(2)}) collective-permute-start(f32[1,32,128,128]{3,2,1,0:T(8,128)S(1)} %get-tuple-element.22), channel_id=1, source_target_pairs={{8,0},{16,8},{24,16},{0,24},{9,1},{17,9},{25,17},{1,25},{10,2},{18... | collective-permute-start | bytes 6291464 | tf_op jit(solution)/shard_map/ppermute | solution.py:17
  550.2 19.6 %copy-start.7 = (f32[1,32,128,128]{3,2,1,0:T(8,128)}, f32[1,32,128,128]{3,2,1,0:T(8,128)S(1)}, u32[]{:S(2)}) copy-start(f32[1,32,128,128]{3,2,1,0:T(8,128)S(1)} %collective-permute-done.18) | copy-start | bytes 6291460
  550.2 12.9 %collective-permute-start.21 = (f32[6,1,128,128]{3,2,1,0:T(8,128)S(1)}, f32[6,1,128,128]{3,2,1,0:T(8,128)S(1)}, u32[]{:S(2)}, u32[]{:S(2)}) collective-permute-start(f32[6,1,128,128]{3,2,1,0:T(8,128)S(1)} %get-tuple-element.13), channel_id=1, source_target_pairs={{0,2},{2,4},{4,6},{6,0},{1,3},{3,5},{5,7},{7,1},{8,10},{10,12},{12... | collective-permute-start | bytes 1179656 | tf_op jit(solution)/shard_map/ppermute | solution.py:16
  551.8 17.9 %collective-permute-start.20 = (f32[6,1,128,128]{3,2,1,0:T(8,128)S(1)}, f32[6,1,128,128]{3,2,1,0:T(8,128)S(1)}, u32[]{:S(2)}, u32[]{:S(2)}) collective-permute-start(f32[6,1,128,128]{3,2,1,0:T(8,128)S(1)} %get-tuple-element.14), channel_id=1, source_target_pairs={{2,0},{4,2},{6,4},{0,6},{3,1},{5,3},{7,5},{1,7},{10,8},{12,10},{14... | collective-permute-start | bytes 1179656 | tf_op jit(solution)/shard_map/ppermute | solution.py:17
  569.8 1.4 collective-permute-start.22
  569.9 1.5 collective-permute-start.23
where the time goes:
time: 603 us
  waiting for transfers between devices  427 us (71%)
  other arithmetic  127 us (21%)
  starting transfers between devices  31.3 us (5%)
  local copies, waits for them, and re-layouts  17.4 us (3%)
    ppermute x12, waiting for transfers between devices, padded(): before = lax.ppermute(last, axis, up)  226 us
    ppermute x12, waiting for transfers between devices, padded(): after = lax.ppermute(leading, axis, down)  201 us
    add x4, other arithmetic, update_lone_timestep(): middle - scaled_wind_second * slopes[0] - scaled_wind_first * slopes[1]  126 us
    ppermute x12, starting transfers between devices, padded(): before = lax.ppermute(last, axis, up)  15.7 us
    ppermute x12, starting transfers between devices, padded(): after = lax.ppermute(leading, axis, down)  15.6 us
  transfers between devices with their start and end apart: 24, of which 24 were waited for; matrix products, arithmetic and copies ran while one was open for 0% of the time, Pallas kernels for 0%

commit v1 on v0

v1 whole, which is shorter than its diff:
```python
import functools

import jax
import jax.numpy as jnp
from jax import lax
from jax.experimental import pallas as pl
from jax.experimental.pallas import tpu as pltpu
from jax.sharding import PartitionSpec as P

STEPS = 4
CHUNKS = 8
TILE = 8
MESH = pl.DeviceIdType.MESH


def beside(axis, shift):
    size = lax.axis_size(axis)
    return {axis: lax.rem(lax.axis_index(axis) + size + shift, size)}


def kernel(
    x, wind_j, wind_i, wind_k, out, state, winds, x_sem, wind_sem, out_sem,
    j_send, j_recv, i_send, i_recv, k_send, k_recv,
):
    J, I, K, _ = x.shape
    width = I // CHUNKS
    inner = pl.ds(TILE, K)
    winds_in = (wind_j, wind_i, wind_k)

    def j_copy(way, step, chunk, first):
        slot, row = lax.rem(step, 2), chunk * width
        if first:
            src = x.at[(J - 1, 0)[way], pl.ds(row, width)]
        else:
            src = state.at[slot, (J, 1)[way], pl.ds(row + 1, width), inner]
        return pltpu.make_async_remote_copy(
            src_ref=src,
            dst_ref=state.at[slot, (0, J + 1)[way], pl.ds(row + 1, width), inner],
            send_sem=j_send.at[way, step, chunk],
            recv_sem=j_recv.at[way, step, chunk],
            device_id=beside("south", (1, -1)[way]),
            device_id_type=MESH,
        )

    def i_copy(way, step, first):
        slot = lax.rem(step, 2)
        if first:
            src = x.at[:, (I - 1, 0)[way]]
        else:
            src = state.at[slot, pl.ds(1, J), (I, 1)[way], inner]
        return pltpu.make_async_remote_copy(
            src_ref=src,
            dst_ref=state.at[slot, pl.ds(1, J), (0, I + 1)[way], inner],
            send_sem=i_send.at[way, step],
            recv_sem=i_recv.at[way, step],
            device_id=beside("east", (1, -1)[way]),
            device_id_type=MESH,
        )

    def k_copy(way, step, chunk, first):
        slot, row = lax.rem(step, 2), chunk * width
        if first:
            src = x.at[:, pl.ds(row, width), pl.ds((K - TILE, 0)[way], TILE)]
        else:
            src = state.at[
                slot, pl.ds(1, J), pl.ds(row + 1, width), pl.ds((K, TILE)[way], TILE)
            ]
        return pltpu.make_async_remote_copy(
            src_ref=src,
            dst_ref=state.at[
                slot, pl.ds(1, J), pl.ds(row + 1, width), pl.ds((0, K + TILE)[way], TILE)
            ],
            send_sem=k_send.at[way, step, chunk],
            recv_sem=k_recv.at[way, step, chunk],
            device_id=beside("down", (1, -1)[way]),
            device_id_type=MESH,
        )

    def x_copy(chunk):
        rows = pl.ds(chunk * width, width)
        return pltpu.make_async_copy(
            x.at[:, rows],
            state.at[0, pl.ds(1, J), pl.ds(chunk * width + 1, width), inner],
            x_sem.at[chunk],
        )

    def wind_copy(which, chunk):
        rows = pl.ds(chunk * width, width)
        return pltpu.make_async_copy(
            winds_in[which].at[:, rows], winds.at[which, :, rows], wind_sem.at[which, chunk]
        )

    def out_copy(chunk):
        rows = pl.ds(chunk * width, width)
        return pltpu.make_async_copy(
            state.at[STEPS % 2, pl.ds(1, J), pl.ds(chunk * width + 1, width), inner],
            out.at[:, rows],
            out_sem.at[chunk],
        )

    def chunk_at(place):
        return jnp.where(lax.rem(place, 2) == 0, place // 2, CHUNKS - 1 - place // 2)

    def send(step, chunk, first):
        for way in (0, 1):
            j_copy(way, step, chunk, first).start()
        for way in (0, 1):
            @pl.when(chunk == (CHUNKS - 1, 0)[way])
            def _():
                i_copy(way, step, first).start()
        for way in (0, 1):
            k_copy(way, step, chunk, first).start()

    def wait_sent(step, chunk, first):
        for way in (0, 1):
            j_copy(way, step, chunk, first).wait_send()
            k_copy(way, step, chunk, first).wait_send()

            @pl.when(chunk == (CHUNKS - 1, 0)[way])
            def _():
                i_copy(way, step, first).wait_send()

    def wait_received(step, chunk):
        for way in (0, 1):
            k_copy(way, step, chunk, False).wait_recv()

            @pl.when(chunk == (0, CHUNKS - 1)[way])
            def _():
                i_copy(way, step, False).wait_recv()

            j_copy(way, step, chunk, False).wait_recv()

    def update(step, chunk):
        now = lax.rem(step, 2)
        later = 1 - now

        def one_row(n, _):
            i = chunk * width + n
            for j in range(1, J + 1):
                middle = state[now, j, i + 1, inner, :]
                j_low, j_high = state[now, j - 1, i + 1, inner, :], state[now, j + 1, i + 1, inner, :]
                i_low, i_high = state[now, j, i, inner, :], state[now, j, i + 2, inner, :]
                k_low = state[now, j, i + 1, pl.ds(TILE - 1, K), :]
                k_high = state[now, j, i + 1, pl.ds(TILE + 1, K), :]
                spread = j_low + j_high + i_low + i_high + k_low + k_high - 6.0 * middle
                state[later, j, i + 1, inner, :] = (
                    middle
                    - winds[0, j - 1, i] * (j_high - j_low)
                    - winds[1, j - 1, i] * (i_high - i_low)
                    - winds[2, j - 1, i] * (k_high - k_low)
                    + 0.05 * spread
                )
            return 0

        lax.fori_loop(0, width, one_row, 0)

    def over(body):
        def one(place, _):
            body(chunk_at(place))
            return 0

        lax.fori_loop(0, CHUNKS, one, 0)

    barrier = pltpu.get_barrier_semaphore()
    for axis in ("south", "east", "down"):
        for shift in (1, -1):
            pl.semaphore_signal(
                barrier, inc=1, device_id=beside(axis, shift), device_id_type=MESH
            )
    over(lambda chunk: x_copy(chunk).start())
    pl.semaphore_wait(barrier, 6)
    over(lambda chunk: send(0, chunk, True))

    def load_winds(chunk):
        for which in range(3):
            wind_copy(which, chunk).start()

    over(load_winds)
    over(lambda chunk: x_copy(chunk).wait())

    def one_step(step, _):
        def one_chunk(chunk):
            @pl.when(step == 0)
            def _():
                for which in range(3):
                    wind_copy(which, chunk).wait()

            @pl.when(step == 1)
            def _():
                wait_sent(0, chunk, True)

            @pl.when(step > 1)
            def _():
                wait_sent(step - 1, chunk, False)

            wait_received(step, chunk)
            update(step, chunk)

            @pl.when(step < STEPS - 1)
            def _():
                send(step + 1, chunk, False)

            @pl.when(step == STEPS - 1)
            def _():
                out_copy(chunk).start()

        over(one_chunk)
        return 0

    lax.fori_loop(0, STEPS, one_step, 0)
    over(lambda chunk: wait_sent(STEPS - 1, chunk, False))
    over(lambda chunk: out_copy(chunk).wait())


def on_device(x, wind_j, wind_i, wind_k):
    J, I, K, L = x.shape
    dma = pltpu.SemaphoreType.DMA
    return pl.pallas_call(
        kernel,
        out_shape=jax.ShapeDtypeStruct(x.shape, x.dtype),
        in_specs=[pl.BlockSpec(memory_space=pl.ANY)] * 4,
        out_specs=pl.BlockSpec(memory_space=pl.ANY),
        scratch_shapes=[
            pltpu.VMEM((2, J + 2, I + 2, K + 2 * TILE, L), x.dtype),
            pltpu.VMEM((3, J, I, K, L), x.dtype),
            dma((CHUNKS,)),
            dma((3, CHUNKS)),
            dma((CHUNKS,)),
            dma((2, STEPS, CHUNKS)),
            dma((2, STEPS, CHUNKS)),
            dma((2, STEPS)),
            dma((2, STEPS)),
            dma((2, STEPS, CHUNKS)),
            dma((2, STEPS, CHUNKS)),
        ],
        compiler_params=pltpu.CompilerParams(
            collective_id=0, has_side_effects=True, vmem_limit_bytes=67043328
        ),
    )(x, wind_j, wind_i, wind_k)


def solution(mesh):
    placed = P("south", "east", "down", None)
    return jax.shard_map(
        on_device, mesh=mesh, in_specs=(placed,) * 4, out_specs=placed, check_vma=False
    )
```

time: 603 us -> 379 us (0.63)
  waiting for transfers between devices: 427 us -> 0 us
  Pallas kernels: 0 us -> 371 us
  other arithmetic: 127 us -> 0 us
  starting transfers between devices: 31.3 us -> 0 us
  local copies, waits for them, and re-layouts: 17.4 us -> 7.89 us
    ppermute x24 -> x0, waiting for transfers between devices: 427 us -> none  [the longest x12 226 us: padded(): before = lax.ppermute(last, axis, up)]
    pallas_call x0 -> x1, Pallas kernels: none -> 371 us  [on_device(): pl.pallas_call(kernel, out_shape=jax.ShapeDtypeStruct(x.shape, x.dtype),...]
    add x4 -> x0, other arithmetic: 126 us -> none  [update_lone_timestep(): middle - scaled_wind_second * slopes[0] - scaled_wind_first * slopes[1]]
    ppermute x24 -> x0, starting transfers between devices: 31.3 us -> none  [the longest x12 15.7 us: padded(): before = lax.ppermute(last, axis, up)]
    slice x13 -> x0, local copies, waits for them, and re-layouts: 12.1 us -> none  [the longest x8 8.03 us: padded(): last = lax.slice_in_dim(array, length - width, length, axis=dim)]
  transfers between devices with their start and end apart: 24 -> 0, of which waited for: 24 -> 0; matrix products, arithmetic and copies ran while one was open for 0% -> 0% of each run, Pallas kernels for 0% -> 0%
where the time goes in v1:
time: 379 us; the launch traced here: 378 us
  Pallas kernels  371 us (98%)
  local copies, waits for them, and re-layouts  7.89 us (2%)
    pallas_call x1, Pallas kernels, on_device(): pl.pallas_call(kernel, out_shape=jax.ShapeDtypeStruct(x.shape, x.dtype),...  371 us
    unnamed x1, local copies, waits for them, and re-layouts  7.89 us

profile of v1, /device:TPU:0, one launch (start us, length us, event | category | flops | bytes accessed | tf_op | source)
XLA Modules:
  0.0 378.4 jit_solution(10366806829810643312)
XLA Ops:
  0.0 370.5 %shard_map.46 = f32[4,32,128,128]{3,2,1,0:T(8,128)} custom-call(f32[4,32,128,128]{3,2,1,0:T(8,128)} %x.1, f32[4,32,128,128]{3,2,1,0:T(8,128)} %wind_j.1, f32[4,32,128,128]{3,2,1,0:T(8,128)} %wind_i.1, f32[4,32,128,128]{3,2,1,0:T(8,128)} %wind_k.1), custom_call_target="tpu_custom_call" | custom-call | tf_op jit(solution)/shard_map/pallas_call | solution.py:218
  370.5 7.9 %copy.6 = f32[4,32,128,128]{3,2,1,0:T(8,128)} copy(f32[4,32,128,128]{3,2,1,0:T(8,128)} %shard_map.46) | data formatting | bytes 16777216

commit v2 on v1

--- a/solution.py
+++ b/solution.py
@@ -8,7 +8,7 @@
 from jax.sharding import PartitionSpec as P
 
 STEPS = 4
-CHUNKS = 8
+CHUNKS = 4
 TILE = 8
 MESH = pl.DeviceIdType.MESH
 
@@ -19,7 +19,7 @@
 
 
 def kernel(
-    x, wind_j, wind_i, wind_k, out, state, winds, x_sem, wind_sem, out_sem,
+    x, wind_j, wind_i, wind_k, out, state, winds, x_sem, wind_sem,
     j_send, j_recv, i_send, i_recv, k_send, k_recv,
 ):
     J, I, K, _ = x.shape
@@ -90,14 +90,6 @@
             winds_in[which].at[:, rows], winds.at[which, :, rows], wind_sem.at[which, chunk]
         )
 
-    def out_copy(chunk):
-        rows = pl.ds(chunk * width, width)
-        return pltpu.make_async_copy(
-            state.at[STEPS % 2, pl.ds(1, J), pl.ds(chunk * width + 1, width), inner],
-            out.at[:, rows],
-            out_sem.at[chunk],
-        )
-
     def chunk_at(place):
         return jnp.where(lax.rem(place, 2) == 0, place // 2, CHUNKS - 1 - place // 2)
 
@@ -130,9 +122,8 @@
 
             j_copy(way, step, chunk, False).wait_recv()
 
-    def update(step, chunk):
+    def update(step, chunk, store):
         now = lax.rem(step, 2)
-        later = 1 - now
 
         def one_row(n, _):
             i = chunk * width + n
@@ -143,12 +134,14 @@
                 k_low = state[now, j, i + 1, pl.ds(TILE - 1, K), :]
                 k_high = state[now, j, i + 1, pl.ds(TILE + 1, K), :]
                 spread = j_low + j_high + i_low + i_high + k_low + k_high - 6.0 * middle
-                state[later, j, i + 1, inner, :] = (
+                store(
+                    j,
+                    i,
                     middle
                     - winds[0, j - 1, i] * (j_high - j_low)
                     - winds[1, j - 1, i] * (i_high - i_low)
                     - winds[2, j - 1, i] * (k_high - k_low)
-                    + 0.05 * spread
+                    + 0.05 * spread,
                 )
             return 0
 
@@ -194,22 +187,27 @@
                 wait_sent(step - 1, chunk, False)
 
             wait_received(step, chunk)
-            update(step, chunk)
 
             @pl.when(step < STEPS - 1)
             def _():
+                def keep(j, i, values):
+                    state[1 - lax.rem(step, 2), j, i + 1, inner, :] = values
+
+                update(step, chunk, keep)
                 send(step + 1, chunk, False)
 
             @pl.when(step == STEPS - 1)
             def _():
-                out_copy(chunk).start()
+                def give(j, i, values):
+                    out[j - 1, i] = values
+
+                update(step, chunk, give)
 
         over(one_chunk)
         return 0
 
     lax.fori_loop(0, STEPS, one_step, 0)
     over(lambda chunk: wait_sent(STEPS - 1, chunk, False))
-    over(lambda chunk: out_copy(chunk).wait())
 
 
 def on_device(x, wind_j, wind_i, wind_k):
@@ -217,15 +215,14 @@
     dma = pltpu.SemaphoreType.DMA
     return pl.pallas_call(
         kernel,
-        out_shape=jax.ShapeDtypeStruct(x.shape, x.dtype),
+        out_shape=pltpu.VMEM(x.shape, x.dtype),
         in_specs=[pl.BlockSpec(memory_space=pl.ANY)] * 4,
-        out_specs=pl.BlockSpec(memory_space=pl.ANY),
+        out_specs=pl.BlockSpec(memory_space=pltpu.VMEM),
         scratch_shapes=[
             pltpu.VMEM((2, J + 2, I + 2, K + 2 * TILE, L), x.dtype),
             pltpu.VMEM((3, J, I, K, L), x.dtype),
             dma((CHUNKS,)),
             dma((3, CHUNKS)),
-            dma((CHUNKS,)),
             dma((2, STEPS, CHUNKS)),
             dma((2, STEPS, CHUNKS)),
             dma((2, STEPS)),
@@ -234,7 +231,7 @@
             dma((2, STEPS, CHUNKS)),
         ],
         compiler_params=pltpu.CompilerParams(
-            collective_id=0, has_side_effects=True, vmem_limit_bytes=67043328
+            collective_id=0, has_side_effects=True, vmem_limit_bytes=54 * 2**20
         ),
     )(x, wind_j, wind_i, wind_k)
 

time: 379 us -> 372 us (0.982)
  local copies, waits for them, and re-layouts: 7.89 us -> 3.4 us
    unnamed x1, local copies, waits for them, and re-layouts: 7.89 us -> 3.4 us
where the time goes in v2:
time: 372 us
  Pallas kernels  369 us (99%)
    pallas_call x1, Pallas kernels, on_device(): pl.pallas_call(kernel, out_shape=pltpu.VMEM(x.shape, x.dtype), in_specs=[...  369 us

profile of v2, /device:TPU:0, one launch (start us, length us, event | category | flops | bytes accessed | tf_op | source)
XLA Modules:
  0.0 372.0 jit_solution(11935035526662564871)
XLA Ops:
  0.0 368.6 %shard_map.46 = f32[4,32,128,128]{3,2,1,0:T(8,128)S(1)} custom-call(f32[4,32,128,128]{3,2,1,0:T(8,128)} %x.1, f32[4,32,128,128]{3,2,1,0:T(8,128)} %wind_j.1, f32[4,32,128,128]{3,2,1,0:T(8,128)} %wind_i.1, f32[4,32,128,128]{3,2,1,0:T(8,128)} %wind_k.1), custom_call_target="tpu_custom_call" | custom-call | tf_op jit(solution)/shard_map/pallas_call | solution.py:216
  368.6 3.4 copy.6
